TPU v7x, 32 devices: a whole 2x2x4 slice. The times are simulated.
32 devices in a mesh: seg: 4 (over y, x), tile: 8 (over z, core).
Axes of the slice: x: 2, y: 2, z: 4, core: 2. Of those that a mesh axis runs over, the one named last changes fastest.
Arguments:
- starting_warmth: float32 [256, 65536], P('tile', 'seg'), may hold values from 0 to 1
- diffusivity_field: float32 [256, 65536], P('tile', 'seg'), may hold values from 0.1 to 1
- emitter_mask: int32 [256, 65536], P('tile', 'seg'), may hold values 0 or 1
Outputs:
- final_warmth: float32 [256, 65536], P('tile', 'seg')
Inputs may be any that keep to these rules, and one draw needn't show every extreme that they name: `emitter_mask`: nonzero marks a source vertex.
All inputs are finite; a program needn't handle non-finite values. No bound on the sum of `emitter_mask` on one device may be relied on, other than what follows from the above.
Results may differ from a plain program's by a relative error of at most 0.00002.
Values sent between devices are 32-bit elements; how exact they have to be, the bound alone decides.
A program may use at most 128 MiB of HBM per device.

v0:
```python
import functools

import jax
import jax.numpy as jnp
from jax import lax
from jax.experimental import pallas as pl
from jax.experimental.pallas import tpu as pltpu
from jax.sharding import PartitionSpec as P

STEPS = 8
ROUNDS = (4, 4)
DEEP = max(ROUNDS)
STEP_SIZE = 0.24
LANES = 128
SUB = 8
MESH = pl.DeviceIdType.MESH

PAD = 16
TERMS = 4
VMEM_KERNEL = 50 * 1024 * 1024
VMEM_LAST = 8 * 1024 * 1024
TERM_ROWS = 5 * SUB


def kernel(
    sizes, u_hbm, k_hbm, s_hbm, out_hbm,
    u_nat, k_nat, s_nat,
    u_0, u_a, u_b, k_row, s_row, coef,
    col_out, col_in, corner_in, row_out, row_in,
    load_sem, store_sem, col_sems, corner_sems, first_sems, row_sems,
):
    rows, blocks, n_seg, n_tile = sizes
    groups = rows // SUB
    tiles = blocks // SUB
    seg, tile = lax.axis_index("seg"), lax.axis_index("tile")
    lane = lax.broadcasted_iota(jnp.int32, (SUB, LANES), 1)
    sublane = lax.broadcasted_iota(jnp.int32, (SUB, LANES), 0)
    first_lane, last_lane = lane == 0, lane == LANES - 1
    has_side = (seg > 0, seg < n_seg - 1)
    has_row = (tile > 0, tile < n_tile - 1)
    side_step = (-1, 1)
    own_at = PAD + SUB
    halo_at = (PAD, own_at + LANES)
    edge_at = (own_at, own_at + LANES - SUB)
    edge_lane = (first_lane, last_lane)
    edge_id = (0, LANES - 1)
    parts = LANES // SUB
    length = LANES + 2 * SUB + 2 * PAD
    zero = jnp.float32(0.0)

    def both(a, b):
        return jnp.logical_and(a, b)

    barrier = pltpu.get_barrier_semaphore()
    count = jnp.int32(0)
    for ds in (-1, 0, 1):
        for dt in (-1, 0, 1):
            if ds == 0 and dt == 0:
                continue
            there = jnp.bool_(True)
            if ds:
                there = has_side[(ds + 1) // 2]
            if dt:
                there = both(there, has_row[(dt + 1) // 2])
            count = count + there.astype(jnp.int32)

            @pl.when(there)
            def _(ds=ds, dt=dt):
                pl.semaphore_signal(barrier, inc=1, device_id=(seg + ds, tile + dt), device_id_type=MESH)

    span = blocks * SUB
    sources = ((u_hbm, u_nat), (k_hbm, k_nat), (s_hbm, s_nat))
    order = [0, groups - 1] + list(range(1, groups - 1))

    def load(which, g):
        src, dst = sources[which]
        part = pl.ds(g * span, span)
        return pltpu.make_async_copy(src.at[part], dst.at[part], load_sem.at[which, g])

    for g in order:
        for which in range(3):
            load(which, g).start()

    zero_plane = jnp.zeros((SUB, LANES), jnp.float32)
    for side in range(2):
        top = 0 if side == 0 else DEEP + rows

        @pl.when(jnp.logical_not(has_row[side]))
        def _(top=top):
            def clear(j, c):
                at = pl.ds(j * SUB, SUB)
                for d in range(DEEP):
                    for ref in (u_0, k_row, s_row):
                        ref[top + d, at, :] = zero_plane
                return c

            lax.fori_loop(0, length // SUB, clear, 0)

    row_refs = (u_0, k_row, s_row)
    own = pl.ds(own_at, LANES)

    def neighbour_run(end, side):
        return jnp.where(edge_lane[side], zero, pltpu.roll(end, (1, LANES - 1)[side], 1))

    def relayout(g):
        for which in range(3):
            load(which, g).wait()

        def body(r, c):
            at = pl.ds(g * span + r, LANES, stride=SUB)
            row = DEEP + g * SUB + r
            for which, ref in enumerate(row_refs):
                plane = (u_nat, k_nat, s_nat)[which][at, :]
                if which == 2:
                    plane = jnp.where(plane != 0, jnp.float32(1.0), zero)
                plane = plane.T
                ref[row, own, :] = plane
                ref[row, halo_at[0]:halo_at[0] + SUB, :] = neighbour_run(plane[-SUB:], 0)
                ref[row, halo_at[1]:halo_at[1] + SUB, :] = neighbour_run(plane[:SUB], 1)
            return c

        lax.fori_loop(0, SUB, body, 0, unroll=4)


    def first_copy(which, side):
        ref, deep = ((u_0, ROUNDS[0]), (k_row, DEEP), (s_row, DEEP))[which]
        if side == 0:
            src, dst = pl.ds(DEEP, deep), pl.ds(DEEP + rows, deep)
        else:
            src, dst = pl.ds(DEEP + rows - deep, deep), pl.ds(DEEP - deep, deep)
        return pltpu.make_async_remote_copy(
            src_ref=ref.at[src, own], dst_ref=ref.at[dst, own],
            send_sem=first_sems.at[0, which, side], recv_sem=first_sems.at[1, which, 1 - side],
            device_id=(seg, tile + side_step[side]), device_id_type=MESH,
        )

    def first_arrival(which, side):
        ref, deep = ((u_0, ROUNDS[0]), (k_row, DEEP), (s_row, DEEP))[which]
        dst = pl.ds(DEEP - deep, deep) if side == 0 else pl.ds(DEEP + rows, deep)
        return pltpu.make_async_remote_copy(
            src_ref=ref.at[dst, own], dst_ref=ref.at[dst, own],
            send_sem=first_sems.at[0, which, side], recv_sem=first_sems.at[1, which, side],
            device_id=(seg, tile + side_step[side]), device_id_type=MESH,
        )

    relayout(0)
    relayout(groups - 1)
    pl.semaphore_wait(barrier, count)
    for side in range(2):
        @pl.when(has_row[side])
        def _(side=side):
            for which in range(3):
                first_copy(which, side).start()

    def col_copy(side):
        return pltpu.make_async_remote_copy(
            src_ref=col_out.at[side], dst_ref=col_in.at[1 - side],
            send_sem=col_sems.at[0, side], recv_sem=col_sems.at[1, 1 - side],
            device_id=(seg + side_step[side], tile), device_id_type=MESH,
        )

    def corner_copy(side, vert):
        return pltpu.make_async_remote_copy(
            src_ref=col_out.at[side],
            dst_ref=corner_in.at[1 - side, 1 - vert],
            send_sem=corner_sems.at[0, side, vert], recv_sem=corner_sems.at[1, 1 - side, 1 - vert],
            device_id=(seg + side_step[side], tile + side_step[vert]), device_id_type=MESH,
        )

    for g in range(1, groups - 1):
        relayout(g)
    for side in range(2):
        for which, ref in enumerate(row_refs):
            packed = jnp.zeros((SUB, LANES), jnp.float32)
            for r in range(rows):
                end = ref[DEEP + r, edge_at[side]:edge_at[side] + SUB, :]
                packed = jnp.where(lane == r, pltpu.roll(end, (r - edge_id[side]) % LANES, 1), packed)
            col_out[side, which * SUB:(which + 1) * SUB, :] = packed

        @pl.when(has_side[side])
        def _(side=side):
            col_copy(side).start()

        for vert in range(2):
            @pl.when(both(has_side[side], has_row[vert]))
            def _(side=side, vert=vert):
                corner_copy(side, vert).start()

    def unpack(ref, side, packed, pairs):
        at = slice(halo_at[side], halo_at[side] + SUB)
        for r, row in pairs:
            end = pltpu.roll(packed, (edge_id[side] - r) % LANES, 1)
            ref[row, at, :] = jnp.where(edge_lane[side], end, ref[row, at, :])

    half = jnp.float32(0.5 * STEP_SIZE)

    def prepare(lo, hi, first=0, end=parts + 2):
        def body(g, c):
            base = pl.multiple_of(g * SUB, SUB) + PAD
            at = pl.ds(base, SUB)
            cell = base - own_at + sublane
            outside = both(both(seg == 0, first_lane), cell < 0)
            outside = jnp.logical_or(outside, both(both(seg == n_seg - 1, last_lane), cell >= LANES))
            above, here = k_row[DEEP + lo - 1, at, :], k_row[DEEP + lo, at, :]
            for r in range(lo, hi):
                row = DEEP + r
                below = k_row[row + 1, at, :]
                live = both(jnp.logical_not(outside), s_row[row, at, :] == 0.0)
                if r < 0:
                    live = both(live, has_row[0])
                if r >= rows:
                    live = both(live, has_row[1])
                weight = jnp.where(live, half, zero)
                cw = weight * (here + k_row[row, pl.ds(base - 1, SUB), :])
                ce = weight * (here + k_row[row, pl.ds(base + 1, SUB), :])
                cn = weight * (here + above)
                cs = weight * (here + below)
                for i, term in enumerate((ce, cw, cn, cs)):
                    coef[row, pl.ds(pl.multiple_of(g * TERM_ROWS, SUB) + i * SUB, SUB), :] = term
                above, here = here, below
            return c

        lax.fori_loop(first, end, body, 0)

    def advance(step, *ranges):
        src, dst = (u_b, u_a) if step % 2 == 0 else (u_a, u_b)
        src = u_0 if step == 0 else src
        last = step == STEPS - 1

        def body(g, c):
            base = pl.multiple_of(g * SUB, SUB) + PAD
            at = pl.ds(base, SUB)
            for lo, hi in ranges:
                here = src[DEEP + lo, at, :]
                rise = here - src[DEEP + lo - 1, at, :]
                for r in range(lo, hi):
                    row = DEEP + r
                    below = src[row + 1, at, :]
                    ce, cw, cn, cs = (
                        coef[row, pl.ds(pl.multiple_of(g * TERM_ROWS, SUB) + i * SUB, SUB), :] for i in range(TERMS)
                    )
                    fall = below - here
                    new = here + (
                        (cs * fall - cn * rise)
                        + (ce * (src[row, pl.ds(base + 1, SUB), :] - here) + cw * (src[row, pl.ds(base - 1, SUB), :] - here))
                    )
                    if step == 0:
                        new = jnp.where(s_row[row, at, :] != 0.0, jnp.float32(1.0), new)
                    dst[row, at, :] = new
                    here, rise = below, fall
            return c

        lax.fori_loop(1 if last else 0, parts + (1 if last else 2), body, 0, unroll=2 if len(ranges) > 1 else 1)

    def row_copy(which, side):
        d = ROUNDS[which]
        return pltpu.make_async_remote_copy(
            src_ref=row_out.at[which, side, pl.ds(0, d)], dst_ref=row_in.at[which, 1 - side, pl.ds(0, d)],
            send_sem=row_sems.at[0, which, side], recv_sem=row_sems.at[1, which, 1 - side],
            device_id=(seg, tile + side_step[side]), device_id_type=MESH,
        )

    def move_rows(src, src_row, src_at, dst, dst_row, dst_at, d):
        def body(j, c):
            for i in range(d):
                dst[dst_row + i, pl.ds(dst_at + j * SUB, SUB), :] = src[src_row + i, pl.ds(src_at + j * SUB, SUB), :]
            return c

        lax.fori_loop(0, parts + 2, body, 0)

    def store(g):
        done_ref = u_b if STEPS % 2 == 0 else u_a
        return pltpu.make_async_copy(
            done_ref.at[pl.ds(DEEP + g * SUB, SUB), own], out_hbm.at[pl.ds(g * SUB, SUB)], store_sem.at[g]
        )

    done = 0
    prepare(1, rows - 1, 2, parts)
    for side in range(2):
        @pl.when(has_side[side])
        def _(side=side):
            col_copy(1 - side).wait_recv()
            for which, ref in enumerate(row_refs):
                unpack(ref, side, col_in[side, which * SUB:(which + 1) * SUB, :], [(r, DEEP + r) for r in range(rows)])
    prepare(1, rows - 1, 0, 2)
    prepare(1, rows - 1, parts, parts + 2)
    for which, d in enumerate(ROUNDS):
        if which:
            cur = u_a if done % 2 == 1 else u_b
            for side in range(2):
                move_rows(cur, DEEP if side == 0 else DEEP + rows - d, PAD, row_out.at[which, side], 0, 0, d)

                @pl.when(has_row[side])
                def _(which=which, side=side):
                    row_copy(which, side).start()

        for j in range(1, d + 1):
            advance(done + j - 1, (j, rows - j))
        if which == len(ROUNDS) - 1:
            for g in range(1, groups - 1):
                if g * SUB >= d and (g + 1) * SUB <= rows - d:
                    store(g).start()

        if which == 0:
            for side in range(2):
                @pl.when(has_row[side])
                def _(side=side):
                    for w in range(3):
                        first_arrival(w, side).wait_recv()
                        first_copy(w, side).wait_send()

            for vert in range(2):
                top = 0 if vert == 0 else DEEP + rows

                @pl.when(has_row[vert])
                def _(vert=vert, top=top):
                    for ref in row_refs:
                        for i in range(DEEP):
                            for side in range(2):
                                end = ref[top + i, edge_at[1 - side]:edge_at[1 - side] + SUB, :]
                                ref[top + i, halo_at[side]:halo_at[side] + SUB, :] = neighbour_run(end, side)

                for side in range(2):
                    @pl.when(both(has_side[side], has_row[vert]))
                    def _(side=side, vert=vert, top=top):
                        corner_copy(1 - side, 1 - vert).wait_recv()
                        for w, ref in enumerate(row_refs):
                            packed = corner_in[side, vert, w * SUB:(w + 1) * SUB, :]
                            pairs = [((rows - DEEP if vert == 0 else 0) + i, top + i) for i in range(DEEP)]
                            unpack(ref, side, packed, pairs)

            prepare(1 - DEEP, 1)
            prepare(rows - 1, rows + DEEP - 1)
        else:
            for side in range(2):
                top = DEEP - d if side == 0 else DEEP + rows

                @pl.when(has_row[side])
                def _(which=which, side=side, top=top, cur=cur, d=d):
                    row_copy(which, 1 - side).wait_recv()
                    move_rows(row_in.at[which, side], 0, 0, cur, top, PAD, d)

                @pl.when(jnp.logical_not(has_row[side]))
                def _(top=top, cur=cur, d=d):
                    def clear(j, c):
                        for i in range(d):
                            cur[top + i, pl.ds(j * SUB, SUB), :] = zero_plane
                        return c

                    lax.fori_loop(0, length // SUB, clear, 0)

        for j in range(1, d + 1):
            final = done + j == STEPS
            advance(
                done + j - 1,
                (0 if final else j - d, j),
                (rows - j, rows if final else rows - j + d),
            )
        done += d

    for g in range(groups):
        if not (g * SUB >= d and (g + 1) * SUB <= rows - d):
            store(g).start()
    for side in range(2):
        @pl.when(has_side[side])
        def _(side=side):
            col_copy(side).wait_send()

        for vert in range(2):
            @pl.when(both(has_side[side], has_row[vert]))
            def _(side=side, vert=vert):
                corner_copy(side, vert).wait_send()

        @pl.when(has_row[side])
        def _(side=side):
            for which in range(1, len(ROUNDS)):
                row_copy(which, side).wait_send()
    for g in range(groups):
        store(g).wait()


def give_back(planes, out):
    for r in range(SUB):
        out[pl.ds(r, LANES, stride=SUB), :] = planes[r].T


def shards(n_seg, n_tile, warmth, conductivity, sources):
    rows, columns = warmth.shape
    blocks = columns // LANES
    groups = rows // SUB

    def planes(a):
        return a.reshape(groups, SUB, blocks, LANES).transpose(0, 2, 1, 3).reshape(-1, LANES)

    flat = rows * blocks
    f32 = jnp.float32
    length = LANES + 2 * SUB + 2 * PAD
    plane = (rows + 2 * DEEP, length, LANES)
    assert blocks == LANES
    vmem = pltpu.VMEM
    sem = pltpu.SemaphoreType.DMA
    n = len(ROUNDS)
    out = pl.pallas_call(
        functools.partial(kernel, (rows, blocks, n_seg, n_tile)),
        out_shape=jax.ShapeDtypeStruct((rows, LANES, LANES), f32),
        in_specs=[pl.BlockSpec(memory_space=pltpu.HBM)] * 3,
        out_specs=pl.BlockSpec(memory_space=pl.ANY),
        scratch_shapes=[
            vmem((flat, LANES), f32), vmem((flat, LANES), f32), vmem((flat, LANES), sources.dtype),
        ] + [vmem(plane, f32)] * 5 + [
            vmem((rows + 2 * DEEP, (LANES // SUB + 2) * TERM_ROWS, LANES), f32),
            vmem((2, 3 * SUB, LANES), f32), vmem((2, 3 * SUB, LANES), f32),
            vmem((2, 2, 3 * SUB, LANES), f32),
            vmem((n, 2, DEEP, LANES + 2 * SUB, LANES), f32), vmem((n, 2, DEEP, LANES + 2 * SUB, LANES), f32),
            sem((3, groups)), sem((groups,)), sem((2, 2)), sem((2, 2, 2)), sem((2, 3, 2)), sem((2, n, 2)),
        ],
        compiler_params=pltpu.CompilerParams(
            collective_id=0, has_side_effects=True, vmem_limit_bytes=VMEM_KERNEL
        ),
    )(planes(warmth), planes(conductivity), planes(sources))
    out = pl.pallas_call(
        give_back,
        grid=(groups,),
        out_shape=jax.ShapeDtypeStruct((flat, LANES), f32),
        in_specs=[pl.BlockSpec((SUB, LANES, LANES), lambda g: (g, 0, 0))],
        out_specs=pl.BlockSpec((blocks * SUB, LANES), lambda g: (g, 0)),
        compiler_params=pltpu.CompilerParams(vmem_limit_bytes=VMEM_LAST),
    )(out)
    return out.reshape(groups, blocks, SUB, LANES).transpose(0, 2, 1, 3).reshape(rows, columns)


def solution(mesh):
    spec = P("tile", "seg")
    return jax.shard_map(
        functools.partial(shards, mesh.shape["seg"], mesh.shape["tile"]),
        mesh=mesh,
        in_specs=(spec, spec, spec),
        out_specs=spec,
        check_vma=False,
    )
```

profile of v0, /device:TPU:1, one launch (start us, length us, event | category | flops | bytes accessed | tf_op | source)
XLA Modules:
  0.0 26.8 jit_solution(7521366649575028507)
XLA Ops:
  0.0 24.5 %shard_map.37.planes = f32[32,128,128]{2,1,0:T(8,128)S(1)} custom-call(f32[4096,128]{1,0:T(8,128)} %bitcast.20, f32[4096,128]{1,0:T(8,128)} %bitcast.21, s32[4096,128]{1,0:T(8,128)} %bitcast.22), custom_call_target="tpu_custom_call" | custom-call | tf_op jit(solution)/shard_map/pallas_call | solution.py:403
  24.5 2.2 %shard_map.38 = f32[4096,128]{1,0:T(8,128)} custom-call(f32[32,128,128]{2,1,0:T(8,128)S(1)} %shard_map.37.planes), custom_call_target="tpu_custom_call" | custom-call | tf_op jit(solution)/shard_map/pallas_call | solution.py:421
where the time goes:
time: 26.9 us; the launch traced here: 26.8 us
  Pallas kernels  26.8 us (100%)
    pallas_call x1, Pallas kernels, shards(): pl.pallas_call(functools.partial(kernel, (rows, blocks, n_seg, n_tile)),...  24.5 us
    pallas_call x1, Pallas kernels, shards(): pl.pallas_call(give_back, grid=(groups,), out_shape=jax.ShapeDtypeStruct(...  2.23 us

commit v1 on v0

v1 whole, which is shorter than its diff:
```python
import functools

import jax
import jax.numpy as jnp
from jax import lax
from jax.experimental import pallas as pl
from jax.experimental.pallas import tpu as pltpu
from jax.sharding import PartitionSpec as P

STEPS = 8
ROUNDS = (1, 3, 4)
PLAN = (
    ("near", 0), ("far", 0), ("fill", 4), ("near", 1), ("fill", 5), ("far", 1),
    ("fill", 8), ("give", 0), ("near", 2), ("far", 2),
)
assert ROUNDS[0] == 1 and ROUNDS[1] > 1
START = tuple(sum(ROUNDS[:m]) for m in range(len(ROUNDS) + 1))
DEEP = max(ROUNDS)
STEP_SIZE = 0.24
LANES = 128
SUB = 8
MESH = pl.DeviceIdType.MESH

PAD = 16
TERMS = 4
VMEM_KERNEL = 50 * 1024 * 1024
VMEM_LAST = 1024 * 1024
TERM_ROWS = 5 * SUB
FIELDS = 3


def chunks():
    have, found = 0, []
    for d in ROUNDS:
        found.append((have, max(have, d)))
        have = max(have, d)
    return found


CHUNKS = chunks()


def kernel(
    sizes, u_hbm, k_hbm, s_hbm, out,
    u_nat, k_nat, s_nat,
    u_0, u_a, u_b, k_row, w_row, coef,
    marks_in, col_out, col_in, corner_in, packed_ref, row_out, row_in,
    load_sem, edge_sem, col_sems, corner_sems, first_sems, row_sems,
):
    rows, blocks, n_seg, n_tile = sizes
    groups = rows // SUB
    n = len(ROUNDS)
    soon = ROUNDS[1]
    seg, tile = lax.axis_index("seg"), lax.axis_index("tile")
    lane = lax.broadcasted_iota(jnp.int32, (SUB, LANES), 1)
    sublane = lax.broadcasted_iota(jnp.int32, (SUB, LANES), 0)
    first_lane, last_lane = lane == 0, lane == LANES - 1
    has_side = (seg > 0, seg < n_seg - 1)
    has_row = (tile > 0, tile < n_tile - 1)
    side_step = (-1, 1)
    own_at = PAD + SUB
    halo_at = (PAD, own_at + LANES)
    edge_at = (own_at, own_at + LANES - SUB)
    edge_lane = (first_lane, last_lane)
    edge_id = (0, LANES - 1)
    parts = LANES // SUB
    length = LANES + 2 * SUB + 2 * PAD
    zero, half = jnp.float32(0.0), jnp.float32(0.5 * STEP_SIZE)
    own = pl.ds(own_at, LANES)
    wide = pl.ds(PAD, LANES + 2 * SUB)
    per_group = FIELDS * SUB
    near = 1 - tile % 2
    far = tile % 2

    def both(a, b):
        return jnp.logical_and(a, b)

    def there_is(side):
        other = tile + 2 * side - 1
        return both(other >= 0, other < n_tile)

    def pick(side, a, b):
        return a + side * (b - a)

    def span_at(side, lo, hi):
        return pick(side, DEEP + lo, DEEP + rows - hi)

    def row_at(side, r):
        return pick(side, DEEP + r, DEEP + rows - 1 - r)

    barrier = pltpu.get_barrier_semaphore()
    count = jnp.int32(0)
    for ds in (-1, 0, 1):
        for dt in (-1, 0, 1):
            if ds == 0 and dt == 0:
                continue
            there = jnp.bool_(True)
            if ds:
                there = has_side[(ds + 1) // 2]
            if dt:
                there = both(there, has_row[(dt + 1) // 2])
            count = count + there.astype(jnp.int32)

            @pl.when(there)
            def _(ds=ds, dt=dt):
                pl.semaphore_signal(barrier, inc=1, device_id=(seg + ds, tile + dt), device_id_type=MESH)

    span = blocks * SUB
    sources = ((u_hbm, u_nat), (k_hbm, k_nat), (s_hbm, s_nat))

    def load(which, g):
        src, dst = sources[which]
        return pltpu.make_async_copy(src.at[g], dst.at[g], load_sem.at[which, g])

    def edge_load(which, side):
        at = pl.ds(0 if side == 0 else (blocks - 1) * SUB, SUB)
        dst = marks_in.at[side] if which == 2 else col_out.at[side, which]
        return pltpu.make_async_copy(sources[which][0].at[:, at], dst, edge_sem.at[which, side])

    for side in range(2):
        for which in range(3):
            edge_load(which, side).start()

    for which in range(2):
        for g in (0, groups - 1):
            load(which, g).start()

    zero_plane = jnp.zeros((SUB, LANES), jnp.float32)
    for side in range(2):
        top = 0 if side == 0 else DEEP + rows

        @pl.when(jnp.logical_not(has_row[side]))
        def _(top=top):
            def clear(j, c):
                at = pl.ds(j * SUB, SUB)
                for d in range(DEEP):
                    for ref in (u_0, u_a, u_b, k_row):
                        ref[top + d, at, :] = zero_plane
                    w_row[top + d, at, :] = zero_plane + half
                return c

            lax.fori_loop(0, length // SUB, clear, 0)

    def relay_heat(row, g, at):
        u_0[DEEP + row, own, :] = u_nat[g, at, :].T

    def relay_rest(row, g, at):
        k = k_nat[g, at, :]
        marked = jnp.where(s_nat[g, at, :] != 0, -k, k).T
        k_row[DEEP + row, own, :] = jnp.abs(marked)
        w_row[DEEP + row, own, :] = jnp.where(marked < 0.0, zero, half)

    def place(row):
        return row, row // SUB, pl.ds(row % SUB, LANES, stride=SUB)

    def relay_k(row, g, at):
        k_row[DEEP + row, own, :] = k_nat[g, at, :].T

    def relay_mark(row, g, at):
        w_row[DEEP + row, own, :] = jnp.where(s_nat[g, at, :] != 0, zero, half).T

    def pair(r):
        return place(r), place(rows - 1 - r)

    def relay_range(relay, lo):
        amount = rows - 2 * lo
        step = max(d for d in range(1, 16) if amount % d == 0)

        def body(i, c):
            for q in range(step):
                relay(*place(lo + i * step + q))
            return c

        lax.fori_loop(0, amount // step, body, 0)

    def first_copy(m, which, side, arriving):
        lo, hi = CHUNKS[m]
        if which == 0:
            ref, lo, hi = u_0, 0, ROUNDS[0]
        elif which == 1:
            ref = k_row
        else:
            ref, lo, hi = w_row, max(lo - 1, 0), hi - 1
        if hi <= lo:
            return None
        mine = span_at(side, lo, hi)
        theirs = pick(side, DEEP + rows + lo, DEEP - hi)
        halo = pick(side, DEEP - hi, DEEP + rows + lo)
        src = ref.at[pl.ds(halo if arriving else mine, hi - lo), own]
        dst = ref.at[pl.ds(halo if arriving else theirs, hi - lo), own]
        other = side if arriving else 1 - side
        return pltpu.make_async_remote_copy(
            src_ref=src, dst_ref=dst,
            send_sem=first_sems.at[0, m, which, side], recv_sem=first_sems.at[1, m, which, other],
            device_id=(seg, tile + pick(side, -1, 1)), device_id_type=MESH,
        )

    def first_fields(m):
        return [w for w in range(3) if (w or m == 0) and (w == 0 or CHUNKS[m][1] > CHUNKS[m][0])]

    def first_send(m, side):
        @pl.when(there_is(side))
        def _():
            for which in first_fields(m):
                copy = first_copy(m, which, side, False)
                if copy is not None:
                    copy.start()

    def col_copy(side):
        return pltpu.make_async_remote_copy(
            src_ref=col_out.at[side], dst_ref=col_in.at[1 - side],
            send_sem=col_sems.at[0, side], recv_sem=col_sems.at[1, 1 - side],
            device_id=(seg + side_step[side], tile), device_id_type=MESH,
        )

    def corner_copy(side, vert):
        g = 0 if vert == 0 else groups - 1
        return pltpu.make_async_remote_copy(
            src_ref=col_out.at[side, :, g], dst_ref=corner_in.at[1 - side, 1 - vert],
            send_sem=corner_sems.at[0, side, vert], recv_sem=corner_sems.at[1, 1 - side, 1 - vert],
            device_id=(seg + side_step[side], tile + side_step[vert]), device_id_type=MESH,
        )

    for g in (0, groups - 1):
        load(2, g).start()
    for which in range(3):
        for g in range(1, groups - 1):
            load(which, g).start()

    for side in range(2):
        for which in range(3):
            edge_load(which, side).wait()
        for g in range(groups):
            col_out[side, 2, g] = jnp.where(marks_in[side, g] != 0, zero, half)
    pl.semaphore_wait(barrier, count)
    for side in range(2):
        @pl.when(has_side[side])
        def _(side=side):
            col_copy(side).start()

        for vert in range(2):
            @pl.when(both(has_side[side], has_row[vert]))
            def _(side=side, vert=vert):
                corner_copy(side, vert).start()

    ends = (0, groups - 1)
    for which in range(2):
        for g in ends:
            load(which, g).wait()
    for where in pair(0):
        relay_heat(*where)
        relay_k(*where)
    for side in range(2):
        first_send(0, side)
    for g in ends:
        load(2, g).wait()
    for where in pair(0):
        relay_mark(*where)
    for r in range(1, soon):
        for where in pair(r):
            relay_rest(*where)
    for side in range(2):
        first_send(1, side)
    for r in range(1, soon + 1):
        for where in pair(r):
            relay_heat(*where)
    for where in pair(soon):
        relay_rest(*where)
    for which in range(3):
        for g in range(1, groups - 1):
            load(which, g).wait()
    relay_range(relay_heat, soon + 1)
    relay_range(relay_rest, soon + 1)

    def prepare(start, amount, halo=None, first=0, end=parts + 2, unroll=1, inner=False):
        def body(g, c):
            base = pl.multiple_of(g * SUB, SUB) + PAD
            at = pl.ds(base, SUB)
            if not inner:
                cell = base - own_at + sublane
                outside = both(both(seg == 0, first_lane), cell < 0)
                outside = jnp.logical_or(outside, both(both(seg == n_seg - 1, last_lane), cell >= LANES))
                inside = jnp.logical_not(outside)
            here = k_row[start, at, :]
            north = here + k_row[start - 1, at, :]
            for i in range(amount):
                row = start + i
                below = k_row[row + 1, at, :]
                weight = w_row[row, at, :]
                if not inner:
                    live = inside
                    if halo is not None:
                        live = both(live, halo(i))
                    weight = jnp.where(live, weight, zero)
                south = here + below
                cw = weight * (here + k_row[row, pl.ds(base - 1, SUB), :])
                ce = weight * (here + k_row[row, pl.ds(base + 1, SUB), :])
                for t, term in enumerate((ce, cw, weight * north, weight * south)):
                    coef[row, pl.ds(pl.multiple_of(g * TERM_ROWS, SUB) + t * SUB, SUB), :] = term
                here, north = below, south
            return c

        lax.fori_loop(first, end, body, 0, unroll=unroll)

    def field(level):
        return u_0 if level == 0 else (u_a if level % 2 == 1 else u_b)

    def advance(j, ranges, unroll=1, first=None, end=None):
        src, dst = field(j - 1), field(j)
        last = j == STEPS

        def body(g, c):
            base = pl.multiple_of(g * SUB, SUB) + PAD
            at = pl.ds(base, SUB)
            for start, amount in ranges:
                here = src[start, at, :]
                rise = here - src[start - 1, at, :]
                for i in range(amount):
                    row = start + i
                    below = src[row + 1, at, :]
                    ce, cw, cn, cs = (
                        coef[row, pl.ds(pl.multiple_of(g * TERM_ROWS, SUB) + t * SUB, SUB), :] for t in range(TERMS)
                    )
                    fall = below - here
                    new = here + (
                        (cs * fall - cn * rise)
                        + (ce * (src[row, pl.ds(base + 1, SUB), :] - here) + cw * (src[row, pl.ds(base - 1, SUB), :] - here))
                    )
                    if j == 1:
                        new = jnp.where(w_row[row, at, :] == 0.0, jnp.float32(1.0), new)
                    dst[row, at, :] = new
                    here, rise = below, fall
            return c

        first = (1 if last else 0) if first is None else first
        end = parts + (1 if last else 2) if end is None else end
        lax.fori_loop(first, end, body, 0, unroll=unroll)

    prepare(DEEP + 1, rows - 2, first=2, end=parts, inner=True)
    advance(1, [(DEEP + 1, rows - 2)], first=2, end=parts)

    row_refs = (u_0, k_row, w_row)

    absent = jnp.where((lane // SUB) % FIELDS == FIELDS - 1, half, zero)
    absent_col = jnp.where(lane >= (FIELDS - 1) * rows, half, zero)

    def packed_of(ref, side):
        a, b = ref.shape[1:3]
        tiles_of = [ref[side, p, q] for p in range(a) for q in range(b)]
        turned = jnp.concatenate(tiles_of + [zero_plane] * (parts - a * b)).T
        return turned[-SUB:] if side == 0 else turned[:SUB]

    def patch(ref, row, side, packed, at_lane):
        end = ref[row, edge_at[1 - side]:edge_at[1 - side] + SUB, :]
        end = pltpu.roll(end, (1, LANES - 1)[side], 1)
        got = pltpu.roll(packed, (edge_id[side] - at_lane) % LANES, 1)
        ref[row, halo_at[side]:halo_at[side] + SUB, :] = jnp.where(edge_lane[side], got, end)

    for side in range(2):
        @pl.when(has_side[side])
        def _(side=side):
            col_copy(1 - side).wait_recv()
    packed_col = [jnp.where(has_side[side], packed_of(col_in, side), absent_col) for side in range(2)]

    def patch_rows(which_rows):
        for side in range(2):
            for r in which_rows:
                for which, ref in enumerate(row_refs):
                    patch(ref, DEEP + r, side, packed_col[side], which * rows + r)

    def sides_of(start, amount):
        for first, end in ((0, 2), (parts, parts + 2)):
            prepare(start, amount, first=first, end=end, unroll=2 if amount < SUB else 1)
            advance(1, [(start, amount)], first=first, end=end, unroll=2 if amount < SUB else 1)

    at_ends = list(range(soon + 1))
    patch_rows(at_ends + [rows - 1 - r for r in at_ends])
    for side in range(2):
        sides_of(span_at(side, 1, soon), soon - 1)

    def row_copy(m, side, early, arriving=False):
        cut = min(ROUNDS[m - 1], ROUNDS[m])
        part = pl.ds(cut, ROUNDS[m] - cut) if early else pl.ds(0, cut)
        other = side if arriving else 1 - side
        return pltpu.make_async_remote_copy(
            src_ref=row_out.at[m - 1, side, part], dst_ref=row_in.at[m - 1, other, part],
            send_sem=row_sems.at[0, m - 1, side, int(early)], recv_sem=row_sems.at[1, m - 1, other, int(early)],
            device_id=(seg, tile + pick(side, -1, 1)), device_id_type=MESH,
        )

    def is_early(m):
        return ROUNDS[m] > ROUNDS[m - 1]

    def row_send(m, side, early):
        cut = min(ROUNDS[m - 1], ROUNDS[m])
        src = field(START[m])

        @pl.when(there_is(side))
        def _():
            for r in range(cut, ROUNDS[m]) if early else range(cut):
                row_out[m - 1, side, r, :, :] = src[row_at(side, r), wide, :]
            row_copy(m, side, early).start()

    def row_take(m, side):
        dst = field(START[m])

        @pl.when(there_is(side))
        def _():
            row_copy(m, side, False, True).wait_recv()
            if is_early(m):
                row_copy(m, side, True, True).wait_recv()
            for r in range(ROUNDS[m]):
                dst[row_at(side, -1 - r), wide, :] = row_in[m - 1, side, r, :, :]

    def halo_rows(m, side):
        lo, hi = CHUNKS[m]

        @pl.when(there_is(side))
        def _():
            for which in first_fields(m):
                copy = first_copy(m, which, side, True)
                if copy is not None:
                    copy.wait_recv()
            for side_of in range(2):
                packed = packed_ref[side_of]
                for which, ref in enumerate(row_refs):
                    if which not in first_fields(m):
                        continue
                    a, b = (lo, hi) if which == 1 else (0, ROUNDS[0]) if which == 0 else (max(lo - 1, 0), hi - 1)
                    for r in range(a, b):
                        at_lane = pick(side, SUB - 1 - r, per_group + r) + which * SUB
                        patch(ref, row_at(side, -1 - r), side_of, packed, at_lane)

        low, high = -(hi - 1), (1 if m == 0 else -(lo - 1))
        start, amount = span_at(side, low, high), high - low

        def halo(i):
            is_halo = jnp.logical_or(start + i < DEEP, start + i >= DEEP + rows)
            return jnp.logical_or(jnp.logical_not(is_halo), there_is(side))

        prepare(start, amount, halo, unroll=6)

    done = {1: 1}
    early_sent = {1}

    def note(j, low):
        done[j] = low
        for m in range(1, n):
            if m not in early_sent and is_early(m) and START[m] == j and low <= ROUNDS[m - 1]:
                early_sent.add(m)
                for side in range(2):
                    row_send(m, side, True)

    def step_all(j, low):
        if j not in done:
            advance(j, [(DEEP + low, rows - 2 * low)])
        elif done[j] > low:
            amount = done[j] - low
            advance(j, [(span_at(side, low, done[j]), amount) for side in range(2)], unroll=2)
        note(j, low)

    def give(row):
        out[row // SUB, pl.ds(row % SUB, LANES, stride=SUB), :] = field(STEPS)[DEEP + row, own, :].T

    for side in range(2):
        row_send(1, side, True)

    for side in range(2):
        for vert in range(2):
            @pl.when(both(has_side[side], has_row[vert]))
            def _(side=side, vert=vert):
                corner_copy(1 - side, 1 - vert).wait_recv()
        packed_ref[side] = jnp.where(has_side[side], packed_of(corner_in, side), absent)

    reached = 0
    for what, arg in PLAN:
        if what == "fill":
            for j in range(START[reached] + 1, arg + 1):
                step_all(j, j - START[reached])
        elif what == "give":
            edge = ROUNDS[n - 1]

            def give_more(i, c, edge=edge):
                give(edge + i)
                return c

            lax.fori_loop(0, rows - 2 * edge, give_more, 0, unroll=8 if (rows - 2 * edge) % 8 == 0 else 2)
        else:
            m, side = arg, near if what == "near" else far
            if m:
                row_take(m, side)
            if CHUNKS[m][1] > CHUNKS[m][0]:
                halo_rows(m, side)
            for j in range(START[m] + 1, START[m + 1] + 1):
                low, high = j - START[m + 1], done[j]
                advance(j, [(span_at(side, low, high), high - low)], unroll=6 if j < STEPS else 4)
            if m + 1 < n:
                row_send(m + 1, side, False)
                if m + 2 < n:
                    first_send(m + 2, side)
            else:
                for i in range(ROUNDS[m]):
                    give(span_at(side, 0, ROUNDS[m]) - DEEP + i)
            if what == "far":
                reached = m + 1
                if m == 0:
                    patch_rows(range(soon + 1, rows - soon - 1))
                    sides_of(DEEP + soon, rows - 2 * soon)
                for j in range(START[m] + 1, START[m + 1] + 1):
                    note(j, j - START[m + 1])

    for side in range(2):
        @pl.when(has_side[side])
        def _(side=side):
            col_copy(side).wait_send()

        for vert in range(2):
            @pl.when(both(has_side[side], has_row[vert]))
            def _(side=side, vert=vert):
                corner_copy(side, vert).wait_send()

        @pl.when(has_row[side])
        def _(side=side):
            for m in range(n):
                for which in first_fields(m):
                    copy = first_copy(m, which, side, False)
                    if copy is not None:
                        copy.wait_send()
            for m in range(1, n):
                row_copy(m, side, False).wait_send()
                if is_early(m):
                    row_copy(m, side, True).wait_send()


def write_out(src, dst, sems):
    copies = [pltpu.make_async_copy(src.at[g], dst.at[g], sems.at[g]) for g in range(src.shape[0])]
    for copy in copies:
        copy.start()
    for copy in copies:
        copy.wait()


def shards(n_seg, n_tile, warmth, conductivity, sources):
    rows, columns = warmth.shape
    blocks = columns // LANES
    groups = rows // SUB

    def planes(a):
        return a.reshape(groups, SUB, blocks, LANES).transpose(0, 2, 1, 3).reshape(groups, -1, LANES)

    flat = (groups, SUB * blocks, LANES)
    f32 = jnp.float32
    length = LANES + 2 * SUB + 2 * PAD
    plane = (rows + 2 * DEEP, length, LANES)
    assert blocks == LANES
    vmem = pltpu.VMEM
    sem = pltpu.SemaphoreType.DMA
    n = len(ROUNDS)
    later = max(n - 1, 1)
    halo = (later, 2, DEEP, LANES + 2 * SUB, LANES)
    out = pl.pallas_call(
        functools.partial(kernel, (rows, blocks, n_seg, n_tile)),
        out_shape=jax.ShapeDtypeStruct(flat, f32),
        in_specs=[pl.BlockSpec(memory_space=pltpu.HBM)] * 3,
        out_specs=pl.BlockSpec(memory_space=pltpu.VMEM),
        scratch_shapes=[
            vmem(flat, f32), vmem(flat, f32), vmem(flat, sources.dtype),
        ] + [vmem(plane, f32)] * 5 + [
            vmem((rows + 2 * DEEP, (LANES // SUB + 2) * TERM_ROWS, LANES), f32),
            vmem((2, groups, SUB, LANES), sources.dtype), vmem((2, FIELDS, groups, SUB, LANES), f32),
            vmem((2, FIELDS, groups, SUB, LANES), f32), vmem((2, 2, FIELDS, SUB, LANES), f32), vmem((2, SUB, LANES), f32),
            vmem(halo, f32), vmem(halo, f32),
            sem((3, groups)), sem((3, 2)), sem((2, 2)), sem((2, 2, 2)), sem((2, n, 3, 2)), sem((2, later, 2, 2)),
        ],
        compiler_params=pltpu.CompilerParams(
            collective_id=0, has_side_effects=True, vmem_limit_bytes=VMEM_KERNEL
        ),
    )(planes(warmth), planes(conductivity), planes(sources))
    out = pl.pallas_call(
        write_out,
        out_shape=jax.ShapeDtypeStruct(flat, f32),
        in_specs=[pl.BlockSpec(memory_space=pl.ANY)],
        out_specs=pl.BlockSpec(memory_space=pltpu.HBM),
        scratch_shapes=[sem((groups,))],
        compiler_params=pltpu.CompilerParams(vmem_limit_bytes=VMEM_LAST),
    )(out)
    return out.reshape(groups, blocks, SUB, LANES).transpose(0, 2, 1, 3).reshape(rows, columns)


def solution(mesh):
    spec = P("tile", "seg")
    return jax.shard_map(
        functools.partial(shards, mesh.shape["seg"], mesh.shape["tile"]),
        mesh=mesh,
        in_specs=(spec, spec, spec),
        out_specs=spec,
        check_vma=False,
    )
```

time: 26.9 us -> 22.2 us (0.83)
  Pallas kernels: 26.8 us -> 21.9 us
    pallas_call x1, Pallas kernels: 24.5 us -> 20.6 us  [shards(): pl.pallas_call(functools.partial(kernel, (rows, blocks, n_seg, n_tile)),...]
    pallas_call x1, Pallas kernels: 2.23 us -> 1.35 us  [shards(): pl.pallas_call(write_out, out_shape=jax.ShapeDtypeStruct(flat, f32), in_s...]
where the time goes in v1:
time: 22.2 us; the launch traced here: 22 us
  Pallas kernels  21.9 us (99%)
    pallas_call x1, Pallas kernels, shards(): pl.pallas_call(functools.partial(kernel, (rows, blocks, n_seg, n_tile)),...  20.6 us
    pallas_call x1, Pallas kernels, shards(): pl.pallas_call(write_out, out_shape=jax.ShapeDtypeStruct(flat, f32), in_s...  1.35 us

profile of v1, /device:TPU:1, one launch (start us, length us, event | category | flops | bytes accessed | tf_op | source)
XLA Modules:
  0.0 22.0 jit_solution(16009780785331755849)
XLA Ops:
  0.0 20.6 %shard_map.37.src = f32[4,1024,128]{2,1,0:T(8,128)S(1)} custom-call(f32[4,1024,128]{2,1,0:T(8,128)} %bitcast.20, f32[4,1024,128]{2,1,0:T(8,128)} %bitcast.21, s32[4,1024,128]{2,1,0:T(8,128)} %bitcast.22), custom_call_target="tpu_custom_call" | custom-call | tf_op jit(solution)/shard_map/pallas_call | solution.py:561
  20.6 1.3 %shard_map.38 = f32[4,1024,128]{2,1,0:T(8,128)} custom-call(f32[4,1024,128]{2,1,0:T(8,128)S(1)} %shard_map.37.src), custom_call_target="tpu_custom_call" | custom-call | tf_op jit(solution)/shard_map/pallas_call | solution.py:579

commit v2 on v1

--- a/solution.py
+++ b/solution.py
@@ -10,8 +10,7 @@
 STEPS = 8
 ROUNDS = (1, 3, 4)
 PLAN = (
-    ("near", 0), ("far", 0), ("fill", 4), ("near", 1), ("fill", 5), ("far", 1),
-    ("fill", 8), ("give", 0), ("near", 2), ("far", 2),
+    ("far", 0), ("near", 0), ("fill", 4), ("far", 1), ("near", 1), ("fill", 8), ("give", 0), ("near", 2), ("far", 2),
 )
 assert ROUNDS[0] == 1 and ROUNDS[1] > 1
 START = tuple(sum(ROUNDS[:m]) for m in range(len(ROUNDS) + 1))
@@ -108,21 +107,28 @@
     span = blocks * SUB
     sources = ((u_hbm, u_nat), (k_hbm, k_nat), (s_hbm, s_nat))
 
-    def load(which, g):
+    ends = (0, groups - 1)
+
+    def load(which, g, amount=1):
         src, dst = sources[which]
-        return pltpu.make_async_copy(src.at[g], dst.at[g], load_sem.at[which, g])
+        part = pl.ds(g, amount)
+        sem = load_sem.at[2 + which if amount > 1 else which // 2]
+        return pltpu.make_async_copy(src.at[part], dst.at[part], sem)
+
+    def loaded(ref, sem):
+        pltpu.make_async_copy(ref, ref, sem).wait()
 
     def edge_load(which, side):
         at = pl.ds(0 if side == 0 else (blocks - 1) * SUB, SUB)
         dst = marks_in.at[side] if which == 2 else col_out.at[side, which]
-        return pltpu.make_async_copy(sources[which][0].at[:, at], dst, edge_sem.at[which, side])
+        return pltpu.make_async_copy(sources[which][0].at[:, at], dst, edge_sem.at[which // 2])
 
     for side in range(2):
         for which in range(3):
             edge_load(which, side).start()
 
     for which in range(2):
-        for g in (0, groups - 1):
+        for g in ends:
             load(which, g).start()
 
     zero_plane = jnp.zeros((SUB, LANES), jnp.float32)
@@ -191,12 +197,18 @@
         other = side if arriving else 1 - side
         return pltpu.make_async_remote_copy(
             src_ref=src, dst_ref=dst,
-            send_sem=first_sems.at[0, m, which, side], recv_sem=first_sems.at[1, m, which, other],
+            send_sem=first_sems.at[n, side], recv_sem=first_sems.at[m, other],
             device_id=(seg, tile + pick(side, -1, 1)), device_id_type=MESH,
         )
 
     def first_fields(m):
         return [w for w in range(3) if (w or m == 0) and (w == 0 or CHUNKS[m][1] > CHUNKS[m][0])]
+
+    def rows_in(m, which):
+        lo, hi = CHUNKS[m]
+        if which == 0:
+            return ROUNDS[0] if m == 0 else 0
+        return hi - lo if which == 1 else max(hi - 1, 0) - max(lo - 1, 0)
 
     def first_send(m, side):
         @pl.when(there_is(side))
@@ -206,10 +218,11 @@
                 if copy is not None:
                     copy.start()
 
-    def col_copy(side):
+    def col_copy(side, part):
+        at = (pl.ds(0, 1), pl.ds(groups - 1, 1), pl.ds(1, groups - 2))[part]
         return pltpu.make_async_remote_copy(
-            src_ref=col_out.at[side], dst_ref=col_in.at[1 - side],
-            send_sem=col_sems.at[0, side], recv_sem=col_sems.at[1, 1 - side],
+            src_ref=col_out.at[side, :, at], dst_ref=col_in.at[1 - side, :, at],
+            send_sem=col_sems.at[0, side], recv_sem=col_sems.at[1 + part // 2, 1 - side],
             device_id=(seg + side_step[side], tile), device_id_type=MESH,
         )
 
@@ -221,39 +234,39 @@
             device_id=(seg + side_step[side], tile + side_step[vert]), device_id_type=MESH,
         )
 
-    for g in (0, groups - 1):
+    for g in ends:
         load(2, g).start()
     for which in range(3):
-        for g in range(1, groups - 1):
-            load(which, g).start()
-
-    for side in range(2):
-        for which in range(3):
-            edge_load(which, side).wait()
+        load(which, 1, groups - 2).start()
+
+    loaded(col_out.at[:, pl.ds(0, 2)], edge_sem.at[0])
+    loaded(marks_in, edge_sem.at[1])
+    for side in range(2):
         for g in range(groups):
             col_out[side, 2, g] = jnp.where(marks_in[side, g] != 0, zero, half)
     pl.semaphore_wait(barrier, count)
     for side in range(2):
-        @pl.when(has_side[side])
-        def _(side=side):
-            col_copy(side).start()
-
         for vert in range(2):
+            @pl.when(has_side[side])
+            def _(side=side, vert=vert):
+                col_copy(side, vert).start()
+
             @pl.when(both(has_side[side], has_row[vert]))
             def _(side=side, vert=vert):
                 corner_copy(side, vert).start()
 
-    ends = (0, groups - 1)
-    for which in range(2):
-        for g in ends:
-            load(which, g).wait()
+    for side in range(2):
+        @pl.when(has_side[side])
+        def _(side=side):
+            col_copy(side, 2).start()
+
+    loaded(u_nat.at[pl.ds(0, 4)], load_sem.at[0])
     for where in pair(0):
         relay_heat(*where)
         relay_k(*where)
     for side in range(2):
         first_send(0, side)
-    for g in ends:
-        load(2, g).wait()
+    loaded(s_nat.at[pl.ds(0, 2)], load_sem.at[1])
     for where in pair(0):
         relay_mark(*where)
     for r in range(1, soon):
@@ -267,8 +280,7 @@
     for where in pair(soon):
         relay_rest(*where)
     for which in range(3):
-        for g in range(1, groups - 1):
-            load(which, g).wait()
+        load(which, 1, groups - 2).wait()
     relay_range(relay_heat, soon + 1)
     relay_range(relay_rest, soon + 1)
 
@@ -344,9 +356,11 @@
     absent = jnp.where((lane // SUB) % FIELDS == FIELDS - 1, half, zero)
     absent_col = jnp.where(lane >= (FIELDS - 1) * rows, half, zero)
 
-    def packed_of(ref, side):
+    def packed_of(ref, side, found=None):
         a, b = ref.shape[1:3]
-        tiles_of = [ref[side, p, q] for p in range(a) for q in range(b)]
+        tiles_of = [
+            zero_plane if found is not None and q not in found else ref[side, p, q] for p in range(a) for q in range(b)
+        ]
         turned = jnp.concatenate(tiles_of + [zero_plane] * (parts - a * b)).T
         return turned[-SUB:] if side == 0 else turned[:SUB]
 
@@ -356,13 +370,20 @@
         got = pltpu.roll(packed, (edge_id[side] - at_lane) % LANES, 1)
         ref[row, halo_at[side]:halo_at[side] + SUB, :] = jnp.where(edge_lane[side], got, end)
 
-    for side in range(2):
-        @pl.when(has_side[side])
-        def _(side=side):
-            col_copy(1 - side).wait_recv()
-    packed_col = [jnp.where(has_side[side], packed_of(col_in, side), absent_col) for side in range(2)]
-
-    def patch_rows(which_rows):
+    def col_wait(which, wanted):
+        for side in range(2):
+            @pl.when(has_side[side])
+            def _(side=side):
+                part = pl.ds(0, wanted)
+                pltpu.make_async_remote_copy(
+                    src_ref=col_in.at[side, :, part], dst_ref=col_in.at[side, :, part],
+                    send_sem=col_sems.at[0, side], recv_sem=col_sems.at[which, side],
+                    device_id=(seg + side_step[side], tile), device_id_type=MESH,
+                ).wait_recv()
+
+    col_wait(1, 2)
+    def patch_rows(which_rows, found):
+        packed_col = [jnp.where(has_side[side], packed_of(col_in, side, found), absent_col) for side in range(2)]
         for side in range(2):
             for r in which_rows:
                 for which, ref in enumerate(row_refs):
@@ -374,7 +395,7 @@
             advance(1, [(start, amount)], first=first, end=end, unroll=2 if amount < SUB else 1)
 
     at_ends = list(range(soon + 1))
-    patch_rows(at_ends + [rows - 1 - r for r in at_ends])
+    patch_rows(at_ends + [rows - 1 - r for r in at_ends], ends)
     for side in range(2):
         sides_of(span_at(side, 1, soon), soon - 1)
 
@@ -384,8 +405,16 @@
         other = side if arriving else 1 - side
         return pltpu.make_async_remote_copy(
             src_ref=row_out.at[m - 1, side, part], dst_ref=row_in.at[m - 1, other, part],
-            send_sem=row_sems.at[0, m - 1, side, int(early)], recv_sem=row_sems.at[1, m - 1, other, int(early)],
+            send_sem=row_sems.at[0, m - 1, side], recv_sem=row_sems.at[1, m - 1, other],
             device_id=(seg, tile + pick(side, -1, 1)), device_id_type=MESH,
+        )
+
+    def row_whole(m, side):
+        part = pl.ds(0, ROUNDS[m])
+        return pltpu.make_async_remote_copy(
+            src_ref=row_out.at[m - 1, side, part], dst_ref=row_in.at[m - 1, side, part],
+            send_sem=row_sems.at[0, m - 1, side], recv_sem=row_sems.at[1, m - 1, side],
+            device_id=(seg, tile + 2 * side - 1), device_id_type=MESH,
         )
 
     def is_early(m):
@@ -406,9 +435,7 @@
 
         @pl.when(there_is(side))
         def _():
-            row_copy(m, side, False, True).wait_recv()
-            if is_early(m):
-                row_copy(m, side, True, True).wait_recv()
+            row_whole(m, side).wait_recv()
             for r in range(ROUNDS[m]):
                 dst[row_at(side, -1 - r), wide, :] = row_in[m - 1, side, r, :, :]
 
@@ -417,10 +444,12 @@
 
         @pl.when(there_is(side))
         def _():
-            for which in first_fields(m):
-                copy = first_copy(m, which, side, True)
-                if copy is not None:
-                    copy.wait_recv()
+            total = sum(rows_in(m, which) for which in range(FIELDS))
+            landed = k_row.at[pl.ds(0, total), own]
+            pltpu.make_async_remote_copy(
+                src_ref=landed, dst_ref=landed, send_sem=first_sems.at[n, side], recv_sem=first_sems.at[m, side],
+                device_id=(seg, tile + 2 * side - 1), device_id_type=MESH,
+            ).wait_recv()
             for side_of in range(2):
                 packed = packed_ref[side_of]
                 for which, ref in enumerate(row_refs):
@@ -472,7 +501,7 @@
                 corner_copy(1 - side, 1 - vert).wait_recv()
         packed_ref[side] = jnp.where(has_side[side], packed_of(corner_in, side), absent)
 
-    reached = 0
+    reached, rounds_met = 0, []
     for what, arg in PLAN:
         if what == "fill":
             for j in range(START[reached] + 1, arg + 1):
@@ -484,7 +513,7 @@
                 give(edge + i)
                 return c
 
-            lax.fori_loop(0, rows - 2 * edge, give_more, 0, unroll=8 if (rows - 2 * edge) % 8 == 0 else 2)
+            lax.fori_loop(0, rows - 2 * edge, give_more, 0, unroll=rows - 2 * edge)
         else:
             m, side = arg, near if what == "near" else far
             if m:
@@ -492,7 +521,7 @@
             if CHUNKS[m][1] > CHUNKS[m][0]:
                 halo_rows(m, side)
             for j in range(START[m] + 1, START[m + 1] + 1):
-                low, high = j - START[m + 1], done[j]
+                low, high = j - START[m + 1], j - START[m]
                 advance(j, [(span_at(side, low, high), high - low)], unroll=6 if j < STEPS else 4)
             if m + 1 < n:
                 row_send(m + 1, side, False)
@@ -501,10 +530,12 @@
             else:
                 for i in range(ROUNDS[m]):
                     give(span_at(side, 0, ROUNDS[m]) - DEEP + i)
-            if what == "far":
+            rounds_met.append(m)
+            if rounds_met.count(m) == 2:
                 reached = m + 1
                 if m == 0:
-                    patch_rows(range(soon + 1, rows - soon - 1))
+                    col_wait(2, groups - 2)
+                    patch_rows(range(soon + 1, rows - soon - 1), range(groups))
                     sides_of(DEEP + soon, rows - 2 * soon)
                 for j in range(START[m] + 1, START[m + 1] + 1):
                     note(j, j - START[m + 1])
@@ -512,7 +543,11 @@
     for side in range(2):
         @pl.when(has_side[side])
         def _(side=side):
-            col_copy(side).wait_send()
+            pltpu.make_async_remote_copy(
+                src_ref=col_out.at[side], dst_ref=col_out.at[side],
+                send_sem=col_sems.at[0, side], recv_sem=col_sems.at[1, side],
+                device_id=(seg + side_step[side], tile), device_id_type=MESH,
+            ).wait_send()
 
         for vert in range(2):
             @pl.when(both(has_side[side], has_row[vert]))
@@ -521,15 +556,14 @@
 
         @pl.when(has_row[side])
         def _(side=side):
-            for m in range(n):
-                for which in first_fields(m):
-                    copy = first_copy(m, which, side, False)
-                    if copy is not None:
-                        copy.wait_send()
+            total = sum(rows_in(m, which) for m in range(n) for which in range(FIELDS))
+            gone = k_row.at[pl.ds(0, total), own]
+            pltpu.make_async_remote_copy(
+                src_ref=gone, dst_ref=gone, send_sem=first_sems.at[n, side], recv_sem=first_sems.at[0, side],
+                device_id=(seg, tile + side_step[side]), device_id_type=MESH,
+            ).wait_send()
             for m in range(1, n):
-                row_copy(m, side, False).wait_send()
-                if is_early(m):
-                    row_copy(m, side, True).wait_send()
+                row_whole(m, side).wait_send()
 
 
 def write_out(src, dst, sems):
@@ -570,7 +604,7 @@
             vmem((2, groups, SUB, LANES), sources.dtype), vmem((2, FIELDS, groups, SUB, LANES), f32),
             vmem((2, FIELDS, groups, SUB, LANES), f32), vmem((2, 2, FIELDS, SUB, LANES), f32), vmem((2, SUB, LANES), f32),
             vmem(halo, f32), vmem(halo, f32),
-            sem((3, groups)), sem((3, 2)), sem((2, 2)), sem((2, 2, 2)), sem((2, n, 3, 2)), sem((2, later, 2, 2)),
+            sem((5,)), sem((2,)), sem((3, 2)), sem((2, 2, 2)), sem((n + 1, 2)), sem((2, later, 2)),
         ],
         compiler_params=pltpu.CompilerParams(
             collective_id=0, has_side_effects=True, vmem_limit_bytes=VMEM_KERNEL

time: 22.2 us -> 21 us (0.946)
  Pallas kernels: 21.9 us -> 20.8 us
    pallas_call x1, Pallas kernels: 20.6 us -> 19.5 us  [shards(): pl.pallas_call(functools.partial(kernel, (rows, blocks, n_seg, n_tile)),...]
where the time goes in v2:
time: 21 us; the launch traced here: 20.8 us
  Pallas kernels  20.8 us (99%)
    pallas_call x1, Pallas kernels, shards(): pl.pallas_call(functools.partial(kernel, (rows, blocks, n_seg, n_tile)),...  19.5 us
    pallas_call x1, Pallas kernels, shards(): pl.pallas_call(write_out, out_shape=jax.ShapeDtypeStruct(flat, f32), in_s...  1.35 us

profile of v2, /device:TPU:1, one launch (start us, length us, event | category | flops | bytes accessed | tf_op | source)
XLA Modules:
  0.0 20.8 jit_solution(5631714096976987643)
XLA Ops:
  0.0 19.5 %shard_map.37.src = f32[4,1024,128]{2,1,0:T(8,128)S(1)} custom-call(f32[4,1024,128]{2,1,0:T(8,128)} %bitcast.20, f32[4,1024,128]{2,1,0:T(8,128)} %bitcast.21, s32[4,1024,128]{2,1,0:T(8,128)} %bitcast.22), custom_call_target="tpu_custom_call" | custom-call | tf_op jit(solution)/shard_map/pallas_call | solution.py:595
  19.5 1.3 %shard_map.38 = f32[4,1024,128]{2,1,0:T(8,128)} custom-call(f32[4,1024,128]{2,1,0:T(8,128)S(1)} %shard_map.37.src), custom_call_target="tpu_custom_call" | custom-call | tf_op jit(solution)/shard_map/pallas_call | solution.py:613

commit v3 on v2

--- a/solution.py
+++ b/solution.py
@@ -10,7 +10,7 @@
 STEPS = 8
 ROUNDS = (1, 3, 4)
 PLAN = (
-    ("far", 0), ("near", 0), ("fill", 4), ("far", 1), ("near", 1), ("fill", 8), ("give", 0), ("near", 2), ("far", 2),
+    ("far", 0), ("near", 0), ("fill", 4), ("near", 1), ("far", 1), ("fill", 8), ("give", 0), ("near", 2), ("far", 2),
 )
 assert ROUNDS[0] == 1 and ROUNDS[1] > 1
 START = tuple(sum(ROUNDS[:m]) for m in range(len(ROUNDS) + 1))
@@ -156,6 +156,21 @@
         k_row[DEEP + row, own, :] = jnp.abs(marked)
         w_row[DEEP + row, own, :] = jnp.where(marked < 0.0, zero, half)
 
+    def sign(lo, amount):
+        def body(i, c):
+            at = pl.ds(pl.multiple_of(i * SUB * SUB, SUB), SUB * SUB)
+            for g in range(lo, lo + amount):
+                k = k_nat[g, at, :]
+                k_nat[g, at, :] = jnp.where(s_nat[g, at, :] != 0, -k, k)
+            return c
+
+        lax.fori_loop(0, blocks // SUB, body, 0, unroll=2)
+
+    def relay_signed(row, g, at):
+        marked = k_nat[g, at, :].T
+        k_row[DEEP + row, own, :] = jnp.abs(marked)
+        w_row[DEEP + row, own, :] = jnp.where(marked < 0.0, zero, half)
+
     def place(row):
         return row, row // SUB, pl.ds(row % SUB, LANES, stride=SUB)
 
@@ -279,10 +294,13 @@
             relay_heat(*where)
     for where in pair(soon):
         relay_rest(*where)
+    for g in ends:
+        sign(g, 1)
     for which in range(3):
         load(which, 1, groups - 2).wait()
+    sign(1, groups - 2)
     relay_range(relay_heat, soon + 1)
-    relay_range(relay_rest, soon + 1)
+    relay_range(relay_signed, soon + 1)
 
     def prepare(start, amount, halo=None, first=0, end=parts + 2, unroll=1, inner=False):
         def body(g, c):

time: 21 us -> 20.4 us (0.971)
  Pallas kernels: 20.8 us -> 20.2 us
    pallas_call x1, Pallas kernels: 19.5 us -> 18.9 us  [shards(): pl.pallas_call(functools.partial(kernel, (rows, blocks, n_seg, n_tile)),...]
where the time goes in v3:
time: 20.4 us; the launch traced here: 20.2 us
  Pallas kernels  20.2 us (99%)
    pallas_call x1, Pallas kernels, shards(): pl.pallas_call(functools.partial(kernel, (rows, blocks, n_seg, n_tile)),...  18.9 us
    pallas_call x1, Pallas kernels, shards(): pl.pallas_call(write_out, out_shape=jax.ShapeDtypeStruct(flat, f32), in_s...  1.35 us

profile of v3, /device:TPU:1, one launch (start us, length us, event | category | flops | bytes accessed | tf_op | source)
XLA Modules:
  0.0 20.2 jit_solution(4900239717990202979)
XLA Ops:
  0.0 18.9 %shard_map.37.src = f32[4,1024,128]{2,1,0:T(8,128)S(1)} custom-call(f32[4,1024,128]{2,1,0:T(8,128)} %bitcast.20, f32[4,1024,128]{2,1,0:T(8,128)} %bitcast.21, s32[4,1024,128]{2,1,0:T(8,128)} %bitcast.22), custom_call_target="tpu_custom_call" | custom-call | tf_op jit(solution)/shard_map/pallas_call | solution.py:613
  18.9 1.3 %shard_map.38 = f32[4,1024,128]{2,1,0:T(8,128)} custom-call(f32[4,1024,128]{2,1,0:T(8,128)S(1)} %shard_map.37.src), custom_call_target="tpu_custom_call" | custom-call | tf_op jit(solution)/shard_map/pallas_call | solution.py:631
